TPU v7x, 32 devices: a whole 2x2x4 slice. The times are simulated.
32 devices in a mesh: gx: 4 (over y, x), gy: 2 (over core), gz: 4 (over z).
Axes of the slice: x: 2, y: 2, z: 4, core: 2. Of those that a mesh axis runs over, the one named last changes fastest.
Arguments:
- rhs: float32 [8, 64, 64, 512], P(None, 'gx', 'gy', 'gz'), may hold values from -8 to 8
- stencil: float32 [14, 64, 64, 512], P(None, 'gx', 'gy', 'gz'), may hold values from 0.02 to 1
Outputs:
- solution: float32 [8, 64, 64, 512], P(None, 'gx', 'gy', 'gz')
- residual: float32 [8, 64, 64, 512], P(None, 'gx', 'gy', 'gz')
All inputs are finite; a program needn't handle non-finite values.
Results may differ from a plain program's by a relative error of at most 0.00029.
Values sent between devices are 32-bit elements; how exact they have to be, the bound alone decides.
A program may use at most 128 MiB of HBM per device.

v0:
```python
import jax
import jax.numpy as jnp
from jax import lax
from jax.sharding import PartitionSpec as P

ITERS = 2


FORWARD = [
    (a, b, c) for a in (-1, 0, 1) for b in (-1, 0, 1) for c in (-1, 0, 1) if (a, b, c) > (0, 0, 0)
]


def with_halo(cells, sides, width):
    for axis, dim in sides:
        count = lax.axis_size(axis)
        ends = count - 1
        head = lax.slice_in_dim(cells, 0, width, axis=dim)
        tail = lax.slice_in_dim(cells, cells.shape[dim] - width, cells.shape[dim], axis=dim)
        cells = jnp.concatenate(
            [
                lax.ppermute(tail, axis, [(i, (i + 1) % count) for i in range(ends)]),
                cells,
                lax.ppermute(head, axis, [((i + 1) % count, i) for i in range(ends)]),
            ],
            axis=dim,
        )
    return cells


def window(array, margin, depth, offset):
    result = array
    for place in range(3):
        dim = array.ndim - 3 + place
        inner = array.shape[dim] - 2 * margin
        begin = margin - depth + offset[place]
        result = lax.slice_in_dim(result, begin, begin + inner + 2 * depth, axis=dim)
    return result


def diagonal_field(padded, margin, depth):
    total = window(padded[0], margin, depth, (0, 0, 0))
    total = total + jnp.sum(window(padded[1:], margin, depth, (0, 0, 0)), axis=0)
    for index, offset in enumerate(FORWARD):
        back = (-offset[0], -offset[1], -offset[2])
        total = total + window(padded[index + 1], margin, depth, back)
    return total


def operate(field, fmargin, padded, smargin, diag, depth):
    result = diag[None] * window(field, fmargin, depth, (0, 0, 0))
    for index, offset in enumerate(FORWARD):
        back = (-offset[0], -offset[1], -offset[2])
        ahead_w = window(padded[index + 1], smargin, depth, (0, 0, 0))
        behind_w = window(padded[index + 1], smargin, depth, back)
        result = result - ahead_w[None] * window(field, fmargin, depth, offset)
        result = result - behind_w[None] * window(field, fmargin, depth, back)
    return result


def gram(left, right):
    flat_l = left.reshape(left.shape[0], -1)
    flat_r = right.reshape(right.shape[0], -1)
    return lax.dot_general(
        flat_l,
        flat_r,
        (((1,), (1,)), ((), ())),
        precision=lax.Precision.HIGHEST,
        preferred_element_type=jnp.float32,
    )


def combine(coef, field):
    return jnp.einsum("ij,ixyz->jxyz", coef, field, precision=lax.Precision.HIGHEST)


def small_dot(left, right):
    return jnp.dot(left, right, precision=lax.Precision.HIGHEST)


def solve_spd(matrix, right):
    factor = jnp.linalg.cholesky(matrix)
    return jax.scipy.linalg.cho_solve((factor, True), right)


def joint_sum(residual, direction, image):
    parts = (
        gram(residual, residual),
        gram(direction, image),
        gram(image, residual),
        gram(image, image),
    )
    return lax.psum((parts[0], parts[1], parts[2], parts[3]), ("gx", "gy", "gz"))


def shards(rhs, stencil):
    padded = with_halo(stencil, (("gx", 1), ("gy", 2), ("gz", 3)), 1)
    smargin = 1
    diag_full = diagonal_field(padded, 1, 0)
    direction = rhs
    dmargin = 0
    residual = direction
    rmargin = dmargin
    solution = jnp.zeros_like(rhs)
    norm_now = None
    for step in range(ITERS):
        field = with_halo(direction, (("gx", 1), ("gy", 2), ("gz", 3)), 1)
        fmargin = 1
        depth = 0
        image = operate(field, fmargin, padded, smargin, diag_full, depth)
        dir_here = window(field, fmargin, depth, (0, 0, 0))
        res_here = window(residual, rmargin, depth, (0, 0, 0))
        dir_core = window(dir_here, depth, 0, (0, 0, 0))
        res_core = window(res_here, depth, 0, (0, 0, 0))
        img_core = window(image, depth, 0, (0, 0, 0))
        norm_now, curve, cross, square = joint_sum(res_core, dir_core, img_core)
        alpha = solve_spd(curve, norm_now)
        solution = solution + combine(alpha, dir_core)
        res_here = res_here - combine(alpha, image)
        if step + 1 < ITERS:
            norm_next = (
                norm_now
                - small_dot(alpha.T, cross)
                - small_dot(cross.T, alpha)
                + small_dot(alpha.T, small_dot(square, alpha))
            )
            beta = solve_spd(norm_now, norm_next)
            direction = res_here + combine(beta, dir_here)
            norm_now = norm_next
        residual = res_here
        rmargin = depth
    return (solution, window(residual, rmargin, 0, (0, 0, 0)))


def solution(mesh):
    in_specs = (P(None, "gx", "gy", "gz"), P(None, "gx", "gy", "gz"))
    out_specs = (P(None, "gx", "gy", "gz"), P(None, "gx", "gy", "gz"))
    return jax.shard_map(shards, mesh=mesh, in_specs=in_specs, out_specs=out_specs, check_vma=False)
```

profile of v0, /device:TPU:0, one launch (start us, length us, event | category | flops | bytes accessed | tf_op | source)
XLA Modules:
  0.0 386.3 jit_solution(13203145947799155079)
XLA Ops:
  4.1 4.9 %collective-permute-start.6 = (f32[8,1,32,128]{3,0,2,1:T(8,128)S(1)}, f32[8,1,32,128]{3,0,2,1:T(8,128)S(1)}, u32[]{:S(2)}, u32[]{:S(2)}) collective-permute-start(f32[8,1,32,128]{3,0,2,1:T(8,128)S(1)} %get-tuple-element.64), channel_id=1, source_target_pairs={{0,8},{8,16},{16,24},{1,9},{9,17},{17,25},{2,10},{10,18},{18,26},{... | collective-permute-start | bytes 393224 | tf_op jit(solution)/shard_map/ppermute | solution.py:22
  18.4 9.2 %collective-permute-done.7 = f32[8,1,32,128]{3,0,2,1:T(8,128)S(1)} collective-permute-done((f32[8,1,32,128]{3,0,2,1:T(8,128)S(1)}, f32[8,1,32,128]{3,0,2,1:T(8,128)S(1)}, u32[]{:S(2)}, u32[]{:S(2)}) %collective-permute-start.7) | collective-permute-done | bytes 131104 | tf_op jit(solution)/shard_map/ppermute | solution.py:24
  42.3 4.5 %collective-permute-start.11 = (f32[8,18,34,1]{2,0,3,1:T(8,128)S(1)}, f32[8,18,34,1]{2,0,3,1:T(8,128)S(1)}, u32[]{:S(2)}, u32[]{:S(2)}) collective-permute-start(f32[8,18,34,1]{2,0,3,1:T(8,128)S(1)} %copy.176), channel_id=1, source_target_pairs={{0,1},{1,2},{2,3},{4,5},{5,6},{6,7},{8,9},{9,10},{10,11},{12,13},{... | collective-permute-start | bytes 58760 | tf_op jit(solution)/shard_map/ppermute | solution.py:22
  54.8 5.5 %convolution_bitcast_fusion.5 = f32[8,8]{0,1:T(8,128)} fusion(f32[8,16,32,128]{3,2,1,0:T(8,128)S(1)} %copy-done), kind=kOutput, calls=%fused_computation.145 | convolution fusion | flops 50331648 | bytes 2097408 | tf_op jit(solution)/shard_map/dot_general | solution.py:64
  68.6 5.6 %fusion.103 = (f32[14,18,34,1]{3,2,1,0:T(8,128)}, f32[14,18,34,1]{3,2,1,0:T(8,128)}) fusion(f32[14,18,34,128]{3,2,1,0:T(8,128)S(1)} %pad_maximum_fusion.1), kind=kLoop, calls=%fused_computation.230 | loop fusion | bytes 137088 | tf_op jit(solution)/shard_map/slice | solution.py:19
  74.2 3.9 %copy.164 = f32[14,18,34,1]{2,0,3,1:T(8,128)S(1)} copy(f32[14,18,34,1]{3,2,1,0:T(8,128)} %get-tuple-element.41) | data formatting | bytes 68544 | tf_op jit(solution)/shard_map/slice | solution.py:19
  81.7 3.9 %copy.165 = f32[14,18,34,1]{2,0,3,1:T(8,128)S(1)} copy(f32[14,18,34,1]{3,2,1,0:T(8,128)} %get-tuple-element.42) | data formatting | bytes 68544 | tf_op jit(solution)/shard_map/slice | solution.py:18
  87.2 8.0 %pad_maximum_fusion.2 = (f32[8,18,34,129]{3,0,2,1:T(8,128)}, f32[8,18,34,129]{3,0,2,1:T(8,128)}) fusion(f32[8,18,34,1]{3,0,2,1:T(8,128)} %copy.175, f32[8,18,1,128]{3,0,2,1:T(8,128)S(1)} %collective-permute-done.9, f32[8,18,32,128]{3,0,2,1:T(8,128)} %copy-done.4, f32[8,18,1,128]{3,0,2,1:T(8,128)S(1)} %collective-permute-done.8, f32[8,18,34,1]{3,0,2,1:T(8,128)} %copy.177), kind=kLoop, calls=%fused_computation.2 | loop fusion | flops 3789504 | bytes 7598592 | tf_op jit(solution)/shard_map/concatenate | solution.py:20
  102.2 13.3 %pad_maximum_fusion = f32[14,18,34,130]{3,2,1,0:T(8,128)} fusion(f32[14,18,34,1]{3,2,1,0:T(8,128)} %copy.167, f32[14,18,1,128]{3,2,1,0:T(1,128)S(1)} %copy.163, f32[14,18,32,128]{3,2,1,0:T(8,128)} %copy-done.5, f32[14,18,1,128]{3,2,1,0:T(1,128)S(1)} %copy.162, f32[14,18,34,1]{3,2,1,0:T(8,128)} %copy.166), kind=kLoop, calls=%fused_computation | loop fusion | flops 4455360 | bytes 8910720 | tf_op jit(solution)/shard_map/concatenate | solution.py:20
  115.5 8.0 %slice_bitcast_fusion.13 = (f32[16,34,130]{2,1,0:T(8,128)}, f32[1,16,34,130]{3,2,1,0:T(8,128)S(1)}, f32[1,16,34,130]{3,2,1,0:T(8,128)S(1)}, f32[1,16,34,130]{3,2...) fusion(f32[14,18,34,130]{3,2,1,0:T(8,128)} %pad_maximum_fusion), kind=kLoop, calls=%fused_computation.159 | loop fusion | bytes 10749440 | tf_op jit(solution)/shard_map/slice | solution.py:37
  146.1 31.7 %fusion.17 = f32[8,16,32,128]{3,0,2,1:T(8,128)} fusion(f32[8,18,32,128]{3,0,2,1:T(8,128)} %copy-done.4, f32[8,18,1,128]{3,0,2,1:T(8,128)S(1)} %collective-permute-done.8, f32[8,18,1,128]{3,0,2,1:T(8,128)S(1)} %collective-permute-done.9, f32[8,18,34,129]{3,0,2,1:T(8,128)} %get-tuple-element.52, f32[8,18,34,129]{3,0,2,1:T(8,128)} %get-tuple-element.51, ...), kind=kLoop, calls=%fused_computation.36 | loop fusion | flops 31981568 | bytes 51789824 | tf_op jit(solution)/shard_map/sub | solution.py:57
  177.8 6.7 %fusion.100 = f32[8,8,1,1]{1,0,3,2:T(8,128)S(1)} fusion(f32[8,16,32,128]{3,0,2,1:T(8,128)} %fusion.17, f32[8,16,32,128]{3,2,1,0:T(8,128)S(1)} %copy-done), kind=kOutput, calls=%fused_computation.227 | convolution fusion | flops 50331648 | bytes 4194560 | tf_op jit(solution)/shard_map/dot_general | solution.py:64
  184.6 4.7 %convolution_bitcast_fusion.4 = f32[8,8]{1,0:T(8,128)S(1)} fusion(f32[8,16,32,128]{3,0,2,1:T(8,128)S(1)} %copy-done.2), kind=kOutput, calls=%fused_computation.142 | convolution fusion | flops 50331648 | bytes 2097408 | tf_op jit(solution)/shard_map/dot_general | solution.py:64
  189.3 40.9 %all-reduce.1 = (f32[8,8]{0,1:T(8,128)S(1)}, f32[8,8]{0,1:T(8,128)S(1)}, f32[8,8]{1,0:T(8,128)S(1)}, f32[8,8]{1,0:T(8,128)S(1)}) all-reduce(f32[8,8]{0,1:T(8,128)S(1)} %copy-done.26, f32[8,8]{0,1:T(8,128)S(1)} %bitcast.147, f32[8,8]{1,0:T(8,128)S(1)} %bitcast.148, ...), channel_id=1, replica_groups=mesh['gx'=4,'gy'=2,'gz'=4] {'gx','gy','gz'}, use_global_device_ids=true, to_apply=%region_4.6 | all-reduce | flops 256 | bytes 2048 | tf_op jit(solution)/shard_map/psum | solution.py:93
  236.0 4.7 %convolution_subtract_fusion.1 = f32[8,16,32,128]{3,0,2,1:T(8,128)S(1)} fusion(f32[8,16,32,128]{3,0,2,1:T(8,128)} %fusion.17, f32[8,8]{1,0:T(8,128)S(1)} %fusion.90, f32[8,16,32,128]{3,2,1,0:T(8,128)S(1)} %copy-done), kind=kOutput, calls=%fused_computation.136 | convolution fusion | flops 50855936 | bytes 6291712 | tf_op jit(solution)/shard_map/ij,ixyz->jxyz/dot_general | solution.py:74
  244.8 4.2 %collective-permute-start.12 = (f32[8,1,32,128]{3,0,2,1:T(8,128)S(1)}, f32[8,1,32,128]{3,0,2,1:T(8,128)S(1)}, u32[]{:S(2)}, u32[]{:S(2)}) collective-permute-start(f32[8,1,32,128]{3,0,2,1:T(8,128)S(1)} %get-tuple-element.61), channel_id=1, source_target_pairs={{0,8},{8,16},{16,24},{1,9},{9,17},{17,25},{2,10},{10,18},{18,26},{... | collective-permute-start | bytes 393224 | tf_op jit(solution)/shard_map/ppermute | solution.py:22
  250.3 4.2 %fusion.95 = f32[8,16,32,128]{3,0,2,1:T(8,128)} fusion(f32[8,8]{1,0:T(8,128)S(1)} %fusion.90, f32[8,16,32,128]{3,2,1,0:T(8,128)S(1)} %copy-done.1), kind=kOutput, calls=%fused_computation.213 | convolution fusion | flops 50331648 | bytes 4194560 | tf_op jit(solution)/shard_map/ij,ixyz->jxyz/dot_general | solution.py:74
  258.7 5.3 %convolution_bitcast_fusion.1 = f32[8,8]{1,0:T(8,128)} fusion(f32[8,16,32,128]{3,0,2,1:T(8,128)S(1)} %convolution_subtract_fusion.1), kind=kOutput, calls=%fused_computation.138 | convolution fusion | flops 50331648 | bytes 2097408 | tf_op jit(solution)/shard_map/dot_general | solution.py:64
  275.5 5.2 %collective-permute-start.17 = (f32[8,18,34,1]{2,0,3,1:T(8,128)}, f32[8,18,34,1]{2,0,3,1:T(8,128)}, u32[]{:S(2)}, u32[]{:S(2)}) collective-permute-start(f32[8,18,34,1]{2,0,3,1:T(8,128)} %copy.217), channel_id=1, source_target_pairs={{0,1},{1,2},{2,3},{4,5},{5,6},{6,7},{8,9},{9,10},{10,11},{12,13},{... | collective-permute-start | bytes 58760 | tf_op jit(solution)/shard_map/ppermute | solution.py:22
  290.0 7.8 %pad_maximum_fusion.3 = (f32[8,18,34,129]{3,0,2,1:T(8,128)}, f32[8,18,34,129]{3,0,2,1:T(8,128)}) fusion(f32[8,18,34,1]{3,0,2,1:T(8,128)} %copy.216, f32[8,18,1,128]{3,0,2,1:T(8,128)S(1)} %collective-permute-done.15, f32[8,1,32,128]{3,0,2,1:T(8,128)S(1)} %collective-permute-done.13, f32[8,16,32,128]{3,0,2,1:T(8,128)S(1)} %convolution_add_fusion.1, ...), kind=kLoop, calls=%fused_computation.4 | loop fusion | flops 6315840 | bytes 7598592 | tf_op jit(solution)/shard_map/concatenate | solution.py:20
  297.8 29.8 %fusion.30 = f32[8,16,32,128]{3,0,2,1:T(8,128)} fusion(f32[8,18,34,129]{3,0,2,1:T(8,128)} %get-tuple-element.48, f32[8,18,34,129]{3,0,2,1:T(8,128)} %get-tuple-element.47, f32[8,18,33,128]{3,0,2,1:T(8,128)} %get-tuple-element.56, f32[8,18,33,128]{3,0,2,1:T(8,128)} %get-tuple-element.55, f32[8,16,32,128]{3,0,2,1:T(8,128)S(1)} %convolution_add_fusion.1, ...), kind=kLoop, calls=%fused_computation.50 | loop fusion | flops 28835840 | bytes 61865984 | tf_op jit(solution)/shard_map/sub | solution.py:57
  327.6 6.2 %convolution_bitcast_fusion.2 = f32[8,8]{0,1:T(8,128)S(1)} fusion(f32[8,16,32,128]{3,0,2,1:T(8,128)S(1)} %convolution_add_fusion.1, f32[8,16,32,128]{3,0,2,1:T(8,128)} %fusion.30), kind=kOutput, calls=%fused_computation.139 | convolution fusion | flops 50331648 | bytes 4194560 | tf_op jit(solution)/shard_map/dot_general | solution.py:64
  333.8 38.9 %all-reduce = (f32[8,8]{1,0:T(8,128)S(1)}, f32[8,8]{0,1:T(8,128)S(1)}) all-reduce(f32[8,8]{1,0:T(8,128)S(1)} %copy-done.25, f32[8,8]{0,1:T(8,128)S(1)} %convolution_bitcast_fusion.2), channel_id=1, replica_groups=mesh['gx'=4,'gy'=2,'gz'=4] {'gx','gy','gz'}, use_global_device_ids=true, to_apply=%region_8.11 | all-reduce | flops 128 | bytes 1024 | tf_op jit(solution)/shard_map/psum | solution.py:93
  375.9 4.1 %convolution_subtract_fusion = f32[8,16,32,128]{3,0,2,1:T(8,128)S(1)} fusion(f32[8,16,32,128]{3,0,2,1:T(8,128)} %copy-done.3, f32[8,8,1,1]{0,1,3,2:T(8,128)S(1)} %convolution_bitcast_fusion, f32[8,16,32,128]{3,0,2,1:T(8,128)} %fusion.30), kind=kOutput, calls=%fused_computation.133 | convolution fusion | flops 50855936 | bytes 6291712 | tf_op jit(solution)/shard_map/ij,ixyz->jxyz/dot_general | solution.py:74
  (189 shorter events, 123.2 us)
Async XLA Ops:
  0.6 16.1 %copy-start = (f32[8,16,32,128]{3,2,1,0:T(8,128)S(1)}, f32[8,16,32,128]{3,2,1,0:T(8,128)}, u32[]{:S(2)}) copy-start(f32[8,16,32,128]{3,2,1,0:T(8,128)} %param.5) | copy-start | bytes 6291460
  4.0 12.0 %copy-start.7 = (f32[8,16,32,128]{3,0,2,1:T(8,128)}, f32[8,16,32,128]{3,0,2,1:T(8,128)S(1)}, u32[]{:S(2)}) copy-start(f32[8,16,32,128]{3,0,2,1:T(8,128)S(1)} %copy.170) | copy-start | bytes 6291460
  4.1 12.0 %collective-permute-start.6 = (f32[8,1,32,128]{3,0,2,1:T(8,128)S(1)}, f32[8,1,32,128]{3,0,2,1:T(8,128)S(1)}, u32[]{:S(2)}, u32[]{:S(2)}) collective-permute-start(f32[8,1,32,128]{3,0,2,1:T(8,128)S(1)} %get-tuple-element.64), channel_id=1, source_target_pairs={{0,8},{8,16},{16,24},{1,9},{9,17},{17,25},{2,10},{10,18},{18,26},{... | collective-permute-start | bytes 393224 | tf_op jit(solution)/shard_map/ppermute | solution.py:22
  10.0 36.8 %collective-permute-start = (f32[14,1,32,128]{3,2,1,0:T(8,128)S(1)}, f32[14,1,32,128]{3,2,1,0:T(8,128)S(1)}, u32[]{:S(2)}, u32[]{:S(2)}) collective-permute-start(f32[14,1,32,128]{3,2,1,0:T(8,128)S(1)} %get-tuple-element.46), channel_id=1, source_target_pairs={{0,8},{8,16},{16,24},{1,9},{9,17},{17,25},{2,10},{10,18},{18,26},{... | collective-permute-start | bytes 688136 | tf_op jit(solution)/shard_map/ppermute | solution.py:22
  13.5 35.9 %collective-permute-start.1 = (f32[14,1,32,128]{3,2,1,0:T(8,128)S(1)}, f32[14,1,32,128]{3,2,1,0:T(8,128)S(1)}, u32[]{:S(2)}, u32[]{:S(2)}) collective-permute-start(f32[14,1,32,128]{3,2,1,0:T(8,128)S(1)} %get-tuple-element.45), channel_id=1, source_target_pairs={{8,0},{16,8},{24,16},{9,1},{17,9},{25,17},{10,2},{18,10},{26,18},{... | collective-permute-start | bytes 688136 | tf_op jit(solution)/shard_map/ppermute | solution.py:24
  14.8 12.9 %collective-permute-start.7 = (f32[8,1,32,128]{3,0,2,1:T(8,128)S(1)}, f32[8,1,32,128]{3,0,2,1:T(8,128)S(1)}, u32[]{:S(2)}, u32[]{:S(2)}) collective-permute-start(f32[8,1,32,128]{3,0,2,1:T(8,128)S(1)} %get-tuple-element.63), channel_id=1, source_target_pairs={{8,0},{16,8},{24,16},{9,1},{17,9},{25,17},{10,2},{18,10},{26,18},{... | collective-permute-start | bytes 393224 | tf_op jit(solution)/shard_map/ppermute | solution.py:24
  16.7 13.6 %copy-start.6 = (f32[14,16,32,128]{3,2,1,0:T(8,128)S(1)}, f32[14,16,32,128]{3,2,1,0:T(8,128)}, u32[]{:S(2)}) copy-start(f32[14,16,32,128]{3,2,1,0:T(8,128)} %param.6) | copy-start | bytes 11010052
  27.7 3.7 collective-permute-start.8
  29.0 3.2 collective-permute-start.9
  38.2 22.1 %collective-permute-start.10 = (f32[8,18,34,1]{2,0,3,1:T(8,128)S(1)}, f32[8,18,34,1]{2,0,3,1:T(8,128)S(1)}, u32[]{:S(2)}, u32[]{:S(2)}) collective-permute-start(f32[8,18,34,1]{2,0,3,1:T(8,128)S(1)} %copy.174), channel_id=1, source_target_pairs={{1,0},{2,1},{3,2},{5,4},{6,5},{7,6},{9,8},{10,9},{11,10},{13,12},{... | collective-permute-start | bytes 58760 | tf_op jit(solution)/shard_map/ppermute | solution.py:24
  42.3 20.7 %collective-permute-start.11 = (f32[8,18,34,1]{2,0,3,1:T(8,128)S(1)}, f32[8,18,34,1]{2,0,3,1:T(8,128)S(1)}, u32[]{:S(2)}, u32[]{:S(2)}) collective-permute-start(f32[8,18,34,1]{2,0,3,1:T(8,128)S(1)} %copy.176), channel_id=1, source_target_pairs={{0,1},{1,2},{2,3},{4,5},{5,6},{6,7},{8,9},{9,10},{10,11},{12,13},{... | collective-permute-start | bytes 58760 | tf_op jit(solution)/shard_map/ppermute | solution.py:22
  51.5 14.0 %collective-permute-start.2 = (f32[14,18,1,128]{3,0,2,1:T(8,128)S(1)}, f32[14,18,1,128]{3,0,2,1:T(8,128)S(1)}, u32[]{:S(2)}, u32[]{:S(2)}) collective-permute-start(f32[14,18,1,128]{3,0,2,1:T(8,128)S(1)} %copy.160), channel_id=1, source_target_pairs={{0,4},{1,5},{2,6},{3,7},{8,12},{9,13},{10,14},{11,15},{16,20},{17,... | collective-permute-start | bytes 387080 | tf_op jit(solution)/shard_map/ppermute | solution.py:22
  53.2 12.4 %collective-permute-start.3 = (f32[14,18,1,128]{3,0,2,1:T(8,128)S(1)}, f32[14,18,1,128]{3,0,2,1:T(8,128)S(1)}, u32[]{:S(2)}, u32[]{:S(2)}) collective-permute-start(f32[14,18,1,128]{3,0,2,1:T(8,128)S(1)} %copy.161), channel_id=1, source_target_pairs={{4,0},{5,1},{6,2},{7,3},{12,8},{13,9},{14,10},{15,11},{20,16},{21,... | collective-permute-start | bytes 387080 | tf_op jit(solution)/shard_map/ppermute | solution.py:24
  78.2 17.0 %collective-permute-start.4 = (f32[14,18,34,1]{2,0,3,1:T(8,128)S(1)}, f32[14,18,34,1]{2,0,3,1:T(8,128)S(1)}, u32[]{:S(2)}, u32[]{:S(2)}) collective-permute-start(f32[14,18,34,1]{2,0,3,1:T(8,128)S(1)} %copy.164), channel_id=1, source_target_pairs={{0,1},{1,2},{2,3},{4,5},{5,6},{6,7},{8,9},{9,10},{10,11},{12,13},{... | collective-permute-start | bytes 102824 | tf_op jit(solution)/shard_map/ppermute | solution.py:22
  85.6 13.1 %collective-permute-start.5 = (f32[14,18,34,1]{2,0,3,1:T(8,128)S(1)}, f32[14,18,34,1]{2,0,3,1:T(8,128)S(1)}, u32[]{:S(2)}, u32[]{:S(2)}) collective-permute-start(f32[14,18,34,1]{2,0,3,1:T(8,128)S(1)} %copy.165), channel_id=1, source_target_pairs={{1,0},{2,1},{3,2},{5,4},{6,5},{7,6},{9,8},{10,9},{11,10},{13,12},{... | collective-permute-start | bytes 102824 | tf_op jit(solution)/shard_map/ppermute | solution.py:24
  146.1 31.7 %copy-start.12 = (f32[16,32,128]{2,1,0:T(8,128)}, f32[16,32,128]{2,1,0:T(8,128)S(1)}, u32[]{:S(2)}) copy-start(f32[16,32,128]{2,1,0:T(8,128)S(1)} %get-tuple-element.69) | copy-start | bytes 786436
  177.8 6.7 %copy-start.2 = (f32[8,16,32,128]{3,0,2,1:T(8,128)S(1)}, f32[8,16,32,128]{3,0,2,1:T(8,128)}, u32[]{:S(2)}) copy-start(f32[8,16,32,128]{3,0,2,1:T(8,128)} %fusion.17) | copy-start | bytes 6291460
  240.7 18.0 %copy-start.3 = (f32[8,16,32,128]{3,0,2,1:T(8,128)}, f32[8,16,32,128]{3,0,2,1:T(8,128)S(1)}, u32[]{:S(2)}) copy-start(f32[8,16,32,128]{3,0,2,1:T(8,128)S(1)} %convolution_subtract_fusion.1) | copy-start | bytes 6291460
  244.8 9.7 %collective-permute-start.12 = (f32[8,1,32,128]{3,0,2,1:T(8,128)S(1)}, f32[8,1,32,128]{3,0,2,1:T(8,128)S(1)}, u32[]{:S(2)}, u32[]{:S(2)}) collective-permute-start(f32[8,1,32,128]{3,0,2,1:T(8,128)S(1)} %get-tuple-element.61), channel_id=1, source_target_pairs={{0,8},{8,16},{16,24},{1,9},{9,17},{17,25},{2,10},{10,18},{18,26},{... | collective-permute-start | bytes 393224 | tf_op jit(solution)/shard_map/ppermute | solution.py:22
  249.0 6.9 %collective-permute-start.13 = (f32[8,1,32,128]{3,0,2,1:T(8,128)S(1)}, f32[8,1,32,128]{3,0,2,1:T(8,128)S(1)}, u32[]{:S(2)}, u32[]{:S(2)}) collective-permute-start(f32[8,1,32,128]{3,0,2,1:T(8,128)S(1)} %get-tuple-element.62), channel_id=1, source_target_pairs={{8,0},{16,8},{24,16},{9,1},{17,9},{25,17},{10,2},{18,10},{26,18},{... | collective-permute-start | bytes 393224 | tf_op jit(solution)/shard_map/ppermute | solution.py:24
  255.9 8.1 %collective-permute-start.14 = (f32[8,18,1,128]{3,0,2,1:T(8,128)S(1)}, f32[8,18,1,128]{3,0,2,1:T(8,128)S(1)}, u32[]{:S(2)}, u32[]{:S(2)}) collective-permute-start(f32[8,18,1,128]{3,0,2,1:T(8,128)S(1)} %get-tuple-element.57), channel_id=1, source_target_pairs={{0,4},{1,5},{2,6},{3,7},{8,12},{9,13},{10,14},{11,15},{16,20},{17,... | collective-permute-start | bytes 221192 | tf_op jit(solution)/shard_map/ppermute | solution.py:22
  257.2 6.8 %collective-permute-start.15 = (f32[8,18,1,128]{3,0,2,1:T(8,128)S(1)}, f32[8,18,1,128]{3,0,2,1:T(8,128)S(1)}, u32[]{:S(2)}, u32[]{:S(2)}) collective-permute-start(f32[8,18,1,128]{3,0,2,1:T(8,128)S(1)} %get-tuple-element.58), channel_id=1, source_target_pairs={{4,0},{5,1},{6,2},{7,3},{12,8},{13,9},{14,10},{15,11},{20,16},{21,... | collective-permute-start | bytes 221192 | tf_op jit(solution)/shard_map/ppermute | solution.py:24
  270.7 12.4 %collective-permute-start.16 = (f32[8,18,34,1]{2,0,3,1:T(8,128)}, f32[8,18,34,1]{2,0,3,1:T(8,128)}, u32[]{:S(2)}, u32[]{:S(2)}) collective-permute-start(f32[8,18,34,1]{2,0,3,1:T(8,128)} %copy.215), channel_id=1, source_target_pairs={{1,0},{2,1},{3,2},{5,4},{6,5},{7,6},{9,8},{10,9},{11,10},{13,12},{... | collective-permute-start | bytes 58760 | tf_op jit(solution)/shard_map/ppermute | solution.py:24
  275.5 11.1 %collective-permute-start.17 = (f32[8,18,34,1]{2,0,3,1:T(8,128)}, f32[8,18,34,1]{2,0,3,1:T(8,128)}, u32[]{:S(2)}, u32[]{:S(2)}) collective-permute-start(f32[8,18,34,1]{2,0,3,1:T(8,128)} %copy.217), channel_id=1, source_target_pairs={{0,1},{1,2},{2,3},{4,5},{5,6},{6,7},{8,9},{9,10},{10,11},{12,13},{... | collective-permute-start | bytes 58760 | tf_op jit(solution)/shard_map/ppermute | solution.py:22
  (21 other events, 81.8 us)
where the time goes:
time: 393 us; the launch traced here: 386 us
  other arithmetic  107 us (27%)
  local copies, waits for them, and re-layouts  95.5 us (24%)
  blocking collectives  79.8 us (20%)
  matrix products  48.1 us (12%)
  starting transfers between devices  42.2 us (11%)
  waiting for transfers between devices  11.5 us (3%)
    psum x2, blocking collectives, joint_sum(): lax.psum((parts[0], parts[1], parts[2], parts[3]), ('gx', 'gy', 'gz'))  79.8 us
    sub x2, other arithmetic, operate(): result = result - behind_w[None] * window(field, fmargin, depth, back)  61.5 us
    concatenate x7, other arithmetic, with_halo(): jnp.concatenate([lax.ppermute(tail, axis, [(i, (i + 1) % count) for i in...  34.7 us
    ppermute x9, starting transfers between devices, with_halo(): lax.ppermute(tail, axis, [(i, (i + 1) % count) for i in range(ends)])  30 us
    dot_general x5, matrix products, gram(): lax.dot_general(flat_l, flat_r, (((1,), (1,)), ((), ())), precision=lax.P...  28.4 us
    slice x35, local copies, waits for them, and re-layouts, window(): lax.slice_in_dim(result, begin, begin + inner + 2 * depth, axis=dim)  28.3 us
    dot_general x5, matrix products, combine(): jnp.einsum('ij,ixyz->jxyz', coef, field, precision=lax.Precision.HIGHEST)  17.8 us
    slice x9, local copies, waits for them, and re-layouts, with_halo(): head = lax.slice_in_dim(cells, 0, width, axis=dim)  17.4 us
  transfers between devices with their start and end apart: 18, of which 3 were waited for; matrix products, arithmetic and copies ran while one was open for 16% of the time, Pallas kernels for 0%

commit v1 on v0

v1 whole, which is shorter than its diff:
```python
import jax
import jax.numpy as jnp
from jax import lax
from jax.experimental import pallas as pl
from jax.experimental.pallas import tpu as pltpu
from jax.sharding import PartitionSpec as P

FORWARD = [
    (a, b, c) for a in (-1, 0, 1) for b in (-1, 0, 1) for c in (-1, 0, 1) if (a, b, c) > (0, 0, 0)
]
AXES = ("gx", "gy", "gz")
LO = [k for k, o in enumerate(FORWARD) if o[2] == 1]
HI = [k for k, o in enumerate(FORWARD) if o[2] == -1]
EX = [k for k, o in enumerate(FORWARD) if o[0] == 1]
F32 = jnp.float32


def runs(ks):
    out = []
    for k in ks:
        if out and out[-1][1] == k:
            out[-1][1] = k + 1
        else:
            out.append([k, k + 1])
    return out


def mm(a, b):
    total = a[:, 0:1] * b[0:1, :]
    for k in range(1, 8):
        total = total + a[:, k : k + 1] * b[k : k + 1, :]
    return total


def solve(matrix, right, row):
    aug = matrix + pltpu.roll(right, 8, 1)
    for k in range(8):
        pivot = aug[k : k + 1, :] / aug[k : k + 1, k : k + 1]
        aug = jnp.where(row == k, pivot, aug - aug[:, k : k + 1] * pivot)
    return pltpu.roll(aug, 120, 1)


def transposed(a, row, lane):
    out = jnp.zeros_like(a)
    for i in range(8):
        line = jnp.sum(jnp.where(lane == row, a[:, i : i + 1], 0.0), axis=0, keepdims=True)
        out = out + jnp.where(row == i, line, 0.0)
    return out


def main_kernel(sizes, dims, rhs, sten, q1_out, q2_out, c_out, p0, q0, pm, pp, w, ws, s0, diag, q2,
                zsend, zrecv, wzsend, wzrecv, red, gacc, cur, slot_x, slot_y, slot_z, lsem,
                xs, xr, ars, arr):
    nf, nx, ny = dims
    yb_n = ny // 8
    tall = ny + 16
    tiles = tall // 8
    pos = {a: lax.axis_index(a) for a in AXES}
    lane = lax.broadcasted_iota(jnp.int32, (8, 128), 1)
    row = lax.broadcasted_iota(jnp.int32, (8, 128), 0)
    ys = pl.ds(8, ny)

    loads = [
        pltpu.make_async_copy(rhs, p0.at[:, pl.ds(1, nx), ys], lsem.at[0]),
        pltpu.make_async_copy(sten.at[pl.ds(1, 13)], w.at[:, pl.ds(1, nx), ys], lsem.at[1]),
        pltpu.make_async_copy(sten.at[0], s0, lsem.at[2]),
    ]
    for copy in loads:
        copy.start()

    for buf in (p0, q0):
        for x in (0, nx + 1):
            buf[:, x] = jnp.zeros((nf, tall, 128), F32)
    w[:, 0] = jnp.zeros((13, tall, 128), F32)

    def clear(x, carry):
        for y in (0, ny + 8):
            p0[:, x, y : y + 8] = jnp.zeros((nf, 8, 128), F32)
            q0[:, x, y : y + 8] = jnp.zeros((nf, 8, 128), F32)
            w[:, x, y : y + 8] = jnp.zeros((13, 8, 128), F32)
        return carry

    lax.fori_loop(1, nx + 1, clear, 0)
    zrecv[...] = jnp.zeros(zrecv.shape, F32)
    wzrecv[...] = jnp.zeros(wzrecv.shape, F32)

    barrier = pltpu.get_barrier_semaphore()
    for a in AXES:
        for d in range(1, sizes[a]):
            pl.semaphore_signal(barrier, inc=1, device_id={a: lax.rem(pos[a] + d, sizes[a])},
                                device_id_type=pl.DeviceIdType.MESH)
    pl.semaphore_wait(barrier, sum(sizes[a] - 1 for a in AXES))

    count = [0]

    def shift(axis, up, src, dst):
        n = sizes[axis]
        i = pos[axis]
        slot = count[0]
        count[0] += 1
        copy = pltpu.make_async_remote_copy(
            src_ref=src, dst_ref=dst, send_sem=xs.at[slot], recv_sem=xr.at[slot],
            device_id={axis: lax.rem(i + (1 if up else n - 1), n)},
            device_id_type=pl.DeviceIdType.MESH)
        sends = i < n - 1 if up else i > 0
        gets = i > 0 if up else i < n - 1

        @pl.when(sends)
        def _():
            copy.start()

        def finish():
            @pl.when(sends)
            def _():
                copy.wait_send()

            @pl.when(gets)
            def _():
                copy.wait_recv()

        return finish

    def finish_all(items):
        for f in items:
            f()

    def y_faces(buf):
        return [
            shift("gy", True, buf.at[:, :, pl.ds(ny, 8)], buf.at[:, :, pl.ds(0, 8)]),
            shift("gy", False, buf.at[:, :, pl.ds(8, 8)], buf.at[:, :, pl.ds(ny + 8, 8)]),
        ]

    def pack(buf, depth, first, which):
        n = len(which)

        def take(k_x, yb):
            if which is ALL:
                return buf[:, k_x, yb * 8 : yb * 8 + 8]
            return jnp.concatenate([buf[k : k + 1, k_x, yb * 8 : yb * 8 + 8] for k in which], axis=0)

        def body(x, acc):
            for yb in range(tiles):
                j = x * tiles + yb
                v = pltpu.roll(take(x, yb), lax.rem(j + 128 - first, 128), 2)
                acc = jnp.where((lane == j)[None], v, acc)
            return acc

        return lax.fori_loop(0, depth, body, jnp.zeros((n, 8, 128), F32))

    ALL = list(range(nf))

    def gram(g, u, v):
        def body(x, accs):
            accs = list(accs)
            for yb in range(yb_n):
                ub = u(x, yb)
                vb = v(x, yb)
                for i in range(nf):
                    accs[i] = accs[i] + ub[i : i + 1] * vb[i:]
            return tuple(accs)

        accs = lax.fori_loop(0, nx, body, tuple(jnp.zeros((nf - i, 8, 128), F32) for i in range(nf)))
        red[...] = jnp.zeros(red.shape, F32)
        for i in range(nf):
            red[i, i:nf, :] = jnp.sum(accs[i], axis=1)
        out = jnp.zeros((8, 128), F32)
        for i in range(nf):
            t = jnp.sum(red[i], axis=1, keepdims=True)
            out = out + jnp.where(lane == 8 * g + i, t, 0.0)
            line = jnp.sum(jnp.where(lane == 8 * g + row, t, 0.0), axis=0, keepdims=True)
            out = out + jnp.where((row == i) & (lane > 8 * g + i), line, 0.0)
        if g == 0:
            gacc[...] = out
        else:
            gacc[...] += out

    def own(buf):
        return lambda x, yb: buf[:, x + 1, 8 + yb * 8 : 16 + yb * 8]

    def z_send(buf, e):
        zsend[e, 0] = pack(buf, nx + 2, 127, ALL)
        zsend[e, 1] = pack(buf, nx + 2, 0, ALL)
        return [
            shift("gz", True, zsend.at[e, 0], zrecv.at[e, 0]),
            shift("gz", False, zsend.at[e, 1], zrecv.at[e, 1]),
        ]

    def z_fill(buf, e):
        def body(x, carry):
            for yb in range(tiles):
                j = x * tiles + yb
                v = buf[:, x, yb * 8 : yb * 8 + 8]
                low = pltpu.roll(zrecv[e, 0], lax.rem(128 - j, 128), 2)
                high = pltpu.roll(zrecv[e, 1], 127 - j, 2)
                pm[:, x, yb * 8 : yb * 8 + 8] = jnp.where((lane == 0)[None], low, pltpu.roll(v, 1, 2))
                pp[:, x, yb * 8 : yb * 8 + 8] = jnp.where((lane == 127)[None], high, pltpu.roll(v, 127, 2))
            return carry

        lax.fori_loop(0, nx + 2, body, 0)

    def behind(k, x, yb):
        a, b, c = FORWARD[k]
        src = w if c == 0 else ws
        return src[k, x + 1 - a, 8 + yb * 8 - b : 16 + yb * 8 - b]

    def ahead(k, x, yb):
        return w[k, x + 1, 8 + yb * 8 : 16 + yb * 8]

    def stencil(buf, put):
        views = {0: buf, -1: pm, 1: pp}

        def body(x, carry):
            for yb in range(yb_n):
                y = 8 + yb * 8
                acc = diag[x, yb * 8 : yb * 8 + 8][None] * buf[:, x + 1, y : y + 8]
                for k, (a, b, c) in enumerate(FORWARD):
                    acc = acc - ahead(k, x, yb)[None] * views[c][:, x + 1 + a, y + b : y + b + 8]
                    acc = acc - behind(k, x, yb)[None] * views[-c][:, x + 1 - a, y - b : y - b + 8]
                put(x, yb, acc)
            return carry

        lax.fori_loop(0, nx, body, 0)

    k0, k1 = EX[0], EX[-1] + 1
    phase = [
        shift("gx", True, rhs.at[:, nx - 1], p0.at[:, 0, ys]),
        shift("gx", False, rhs.at[:, 0], p0.at[:, nx + 1, ys]),
        shift("gx", True, sten.at[pl.ds(k0 + 1, k1 - k0), nx - 1], w.at[pl.ds(k0, k1 - k0), 0, ys]),
    ]
    loads[0].wait()
    gram(0, own(p0), own(p0))
    loads[1].wait()
    loads[2].wait()
    finish_all(phase)
    phase = y_faces(p0)
    for b, up, src, dst in ((1, True, ny, 0), (-1, False, 8, ny + 8)):
        for lo, hi in runs([k for k, o in enumerate(FORWARD) if o[1] == b]):
            ks = pl.ds(lo, hi - lo)
            phase.append(shift("gy", up, w.at[ks, :, pl.ds(src, 8)], w.at[ks, :, pl.ds(dst, 8)]))
    finish_all(phase)
    phase = z_send(p0, 0)
    wzsend[0 : len(LO)] = pack(w, nx + 1, 127, LO)
    wzsend[len(LO) : len(LO) + len(HI)] = pack(w, nx + 1, 0, HI)
    lo_part, hi_part = pl.ds(0, len(LO)), pl.ds(len(LO), len(HI))
    phase += [
        shift("gz", True, wzsend.at[lo_part], wzrecv.at[lo_part]),
        shift("gz", False, wzsend.at[hi_part], wzrecv.at[hi_part]),
    ]
    finish_all(phase)
    z_fill(p0, 0)

    def w_fill(x, carry):
        for yb in range(tiles):
            j = x * tiles + yb
            for n, k in enumerate(LO):
                v = pltpu.roll(w[k, x, yb * 8 : yb * 8 + 8], 1, 1)
                ws[k, x, yb * 8 : yb * 8 + 8] = jnp.where(
                    lane == 0, pltpu.roll(wzrecv[n], lax.rem(128 - j, 128), 1), v)
            for n, k in enumerate(HI):
                v = pltpu.roll(w[k, x, yb * 8 : yb * 8 + 8], 127, 1)
                ws[k, x, yb * 8 : yb * 8 + 8] = jnp.where(
                    lane == 127, pltpu.roll(wzrecv[len(LO) + n], 127 - j, 1), v)
        return carry

    lax.fori_loop(0, nx + 1, w_fill, 0)

    def make_diag(x, carry):
        for yb in range(yb_n):
            total = s0[x, yb * 8 : yb * 8 + 8]
            for k in range(13):
                total = total + ahead(k, x, yb) + behind(k, x, yb)
            diag[x, yb * 8 : yb * 8 + 8] = total
        return carry

    lax.fori_loop(0, nx, make_diag, 0)

    def put_q1(x, yb, v):
        q0[:, x + 1, 8 + yb * 8 : 16 + yb * 8] = v

    stencil(p0, put_q1)

    phase = [
        shift("gx", True, q0.at[:, nx, ys], q0.at[:, 0, ys]),
        shift("gx", False, q0.at[:, 1, ys], q0.at[:, nx + 1, ys]),
    ]
    save1 = pltpu.make_async_copy(q0.at[:, pl.ds(1, nx), ys], q1_out, lsem.at[3])
    save1.start()
    gram(1, own(p0), own(q0))
    finish_all(phase)
    phase = y_faces(q0)
    finish_all(phase)
    phase = z_send(q0, 1)
    gram(2, own(q0), own(q0))
    finish_all(phase)
    z_fill(q0, 1)

    def put_q2(x, yb, v):
        q2[:, x, yb * 8 : yb * 8 + 8] = v

    stencil(q0, put_q2)
    save2 = pltpu.make_async_copy(q2, q2_out, lsem.at[4])
    save2.start()
    gram(3, own(q0), lambda x, yb: q2[:, x, yb * 8 : yb * 8 + 8])

    total = gacc[...]
    base = 0
    for stage, (a, slots) in enumerate(zip(("gy", "gx", "gz"), (slot_y, slot_x, slot_z))):
        n = sizes[a]
        i = pos[a]
        cur[stage] = total
        slots[i] = total
        copies = []
        for d in range(1, n):
            copies.append(pltpu.make_async_remote_copy(
                src_ref=cur.at[stage], dst_ref=slots.at[i],
                send_sem=ars.at[base + d - 1], recv_sem=arr.at[base + d - 1],
                device_id={a: lax.rem(i + d, n)}, device_id_type=pl.DeviceIdType.MESH))
        for copy in copies:
            copy.start()
        for d, copy in zip(range(1, n), copies):
            copy.wait_send()
            pltpu.make_async_remote_copy(
                src_ref=cur.at[stage], dst_ref=slots.at[lax.rem(i + n - d, n)],
                send_sem=ars.at[base + d - 1], recv_sem=arr.at[base + d - 1],
                device_id={a: lax.rem(i + d, n)}, device_id_type=pl.DeviceIdType.MESH).wait_recv()
        total = slots[0]
        for s in range(1, n):
            total = total + slots[s]
        base += n - 1

    small = lane < 8
    parts = [jnp.where(small, pltpu.roll(total, (128 - 8 * g) % 128, 1), 0.0) for g in range(4)]
    rr, pq, ss, tt = parts
    alpha = jnp.where(small, solve(pq, rr, row), 0.0)
    alpha_t = transposed(alpha, row, lane)
    alpha_t = jnp.where(small, alpha_t, 0.0)
    ssa = mm(ss, alpha)
    new = rr - mm(alpha_t, pq) - mm(pq, alpha) + mm(alpha_t, ssa)
    beta = jnp.where(small, solve(rr, new, row), 0.0)
    ib = beta + jnp.where(lane == row, 1.0, 0.0)
    ib_t = jnp.where(small, transposed(ib, row, lane), 0.0)
    curve = mm(ib_t, mm(pq, ib) - ssa) - mm(alpha_t, mm(ss, ib) - mm(tt, alpha))
    alpha1 = jnp.where(small, solve(curve, new, row), 0.0)
    c_out[0] = alpha + mm(ib, alpha1)
    c_out[1] = mm(alpha, alpha1)
    save1.wait()
    save2.wait()


def final_kernel(yb_n, xs_n, c, r0, q1, q2, sol, res, table):
    @pl.when(pl.program_id(0) == 0)
    def _():
        for n in range(2):
            for i in range(8):
                for j in range(8):
                    table[n, i, j] = jnp.full((8, 128), c[n, i, j], F32)

    def body(x, carry):
        for yb in range(yb_n):
            y = slice(yb * 8, yb * 8 + 8)
            s = jnp.zeros((8, 8, 128), F32)
            e = r0[:, x, y]
            for i in range(8):
                t1, t2 = table[0, i], table[1, i]
                a, b, d = r0[i, x, y][None], q1[i, x, y][None], q2[i, x, y][None]
                s = s + (t1 * a - t2 * b)
                e = e + (t2 * d - t1 * b)
            sol[:, x, y] = s
            res[:, x, y] = e
        return carry

    lax.fori_loop(0, xs_n, body, 0)


def shards(sizes, rhs, stencil):
    nf, nx, ny, nz = rhs.shape
    tall = ny + 16
    field = jax.ShapeDtypeStruct(rhs.shape, F32)
    anyspace = pl.BlockSpec(memory_space=pl.ANY)
    peers = sum(sizes[a] - 1 for a in AXES)
    padded = pltpu.VMEM((nf, nx + 2, tall, nz), F32)

    def kernel(*refs):
        main_kernel(sizes, (nf, nx, ny), *refs)

    q1, q2, c = pl.pallas_call(
        kernel,
        out_shape=(field, field, jax.ShapeDtypeStruct((2, 8, 128), F32)),
        in_specs=[anyspace, anyspace],
        out_specs=(anyspace, anyspace, pl.BlockSpec(memory_space=pltpu.VMEM)),
        scratch_shapes=[
            padded, padded, padded, padded,
            pltpu.VMEM((13, nx + 1, tall, nz), F32),
            pltpu.VMEM((13, nx + 1, tall, nz), F32),
            pltpu.VMEM((nx, ny, nz), F32),
            pltpu.VMEM((nx, ny, nz), F32),
            pltpu.VMEM((nf, nx, ny, nz), F32),
            pltpu.VMEM((2, 2, nf, 8, nz), F32),
            pltpu.VMEM((2, 2, nf, 8, nz), F32),
            pltpu.VMEM((len(LO) + len(HI), 8, nz), F32),
            pltpu.VMEM((len(LO) + len(HI), 8, nz), F32),
            pltpu.VMEM((8, 8, 128), F32),
            pltpu.VMEM((8, 128), F32),
            pltpu.VMEM((3, 8, 128), F32),
            pltpu.VMEM((sizes["gx"], 8, 128), F32),
            pltpu.VMEM((sizes["gy"], 8, 128), F32),
            pltpu.VMEM((sizes["gz"], 8, 128), F32),
            pltpu.SemaphoreType.DMA((5,)),
            pltpu.SemaphoreType.DMA((24,)),
            pltpu.SemaphoreType.DMA((24,)),
            pltpu.SemaphoreType.DMA((peers,)),
            pltpu.SemaphoreType.DMA((peers,)),
        ],
        compiler_params=pltpu.CompilerParams(
            collective_id=0, has_side_effects=True, vmem_limit_bytes=60 * 2**20),
        name="krylov",
    )(rhs, stencil)

    step = 2
    block = pl.BlockSpec((nf, step, ny, nz), lambda i: (0, i, 0, 0))

    def last(*refs):
        final_kernel(ny // 8, step, *refs)

    return pl.pallas_call(
        last,
        grid=(nx // step,),
        out_shape=(field, field),
        in_specs=[pl.BlockSpec(memory_space=pltpu.SMEM), block, block, block],
        out_specs=(block, block),
        scratch_shapes=[pltpu.VMEM((2, 8, 8, 8, 128), F32)],
        compiler_params=pltpu.CompilerParams(dimension_semantics=("arbitrary",), vmem_limit_bytes=32 * 2**20),
        name="combine",
    )(c, rhs, q1, q2)


def solution(mesh):
    sizes = {a: mesh.shape[a] for a in AXES}
    spec = P(None, "gx", "gy", "gz")

    def run(rhs, stencil):
        return shards(sizes, rhs, stencil)

    return jax.shard_map(run, mesh=mesh, in_specs=(spec, spec), out_specs=(spec, spec), check_vma=False)
```

time: 393 us -> 94.1 us (0.24); the launches traced: 386 us -> 93.9 us
  other arithmetic: 107 us -> 0 us
  local copies, waits for them, and re-layouts: 95.5 us -> 3.88 us
  Pallas kernels: 0 us -> 89.4 us
  blocking collectives: 79.8 us -> 0 us
  matrix products: 48.1 us -> 0 us
  starting transfers between devices: 42.2 us -> 0 us
  waiting for transfers between devices: 11.5 us -> 0 us
    pallas_call x0 -> x2, Pallas kernels: none -> 89.4 us  [the longest x1 82.2 us: shards(): pl.pallas_call(kernel, out_shape=(field, field, jax.ShapeDtypeStruct((2,...]
    psum x2 -> x0, blocking collectives: 79.8 us -> none  [joint_sum(): lax.psum((parts[0], parts[1], parts[2], parts[3]), ('gx', 'gy', 'gz'))]
    slice x51 -> x0, local copies, waits for them, and re-layouts: 61.7 us -> none  [the longest x35 28.3 us: window(): lax.slice_in_dim(result, begin, begin + inner + 2 * depth, axis=dim)]
    sub x2 -> x0, other arithmetic: 61.5 us -> none  [operate(): result = result - behind_w[None] * window(field, fmargin, depth, back)]
    dot_general x14 -> x0, matrix products: 47 us -> none  [the longest x5 28.4 us: gram(): lax.dot_general(flat_l, flat_r, (((1,), (1,)), ((), ())), precision=lax.P...]
    ppermute x18 -> x0, starting transfers between devices: 42.2 us -> none  [the longest x9 30 us: with_halo(): lax.ppermute(tail, axis, [(i, (i + 1) % count) for i in range(ends)])]
    concatenate x7 -> x0, other arithmetic: 34.7 us -> none  [with_halo(): jnp.concatenate([lax.ppermute(tail, axis, [(i, (i + 1) % count) for i in...]
    ppermute x8 -> x0, local copies, waits for them, and re-layouts: 19.4 us -> none  [the longest x4 9.82 us: with_halo(): lax.ppermute(head, axis, [((i + 1) % count, i) for i in range(ends)])]
  transfers between devices with their start and end apart: 18 -> 0, of which waited for: 3 -> 0; matrix products, arithmetic and copies ran while one was open for 16% -> 0% of each run, Pallas kernels for 0% -> 0%
where the time goes in v1:
time: 94.1 us; the launch traced here: 93.9 us
  Pallas kernels  89.4 us (95%)
  local copies, waits for them, and re-layouts  3.88 us (4%)
    pallas_call x1, Pallas kernels, shards(): pl.pallas_call(kernel, out_shape=(field, field, jax.ShapeDtypeStruct((2,...  82.2 us
    pallas_call x1, Pallas kernels, shards(): pl.pallas_call(last, grid=(nx // step,), out_shape=(field, field), in_spe...  7.21 us
    unnamed x8, local copies, waits for them, and re-layouts  3.88 us

profile of v1, /device:TPU:0, one launch (start us, length us, event | category | flops | bytes accessed | tf_op | source)
XLA Modules:
  0.0 93.9 jit_solution(15225407079872875172)
XLA Ops:
  0.6 0.0 copy-start
  0.6 82.2 %krylov.1 = (f32[8,16,32,128]{3,2,1,0:T(8,128)}, f32[8,16,32,128]{3,2,1,0:T(8,128)}, f32[2,8,128]{2,1,0:T(8,128)}) custom-call(f32[8,16,32,128]{3,2,1,0:T(8,128)} %refs_1_.3, f32[14,16,32,128]{3,2,1,0:T(8,128)} %refs_1_.2), custom_call_target="tpu_custom_call" | custom-call | tf_op jit(solution)/shard_map/krylov/pallas_call | solution.py:386
  82.8 0.0 copy-done
  82.8 0.0 copy-start.1
  82.8 1.6 %copy-done.1 = f32[8,16,32,128]{3,2,1,0:T(8,128)S(1)} copy-done((f32[8,16,32,128]{3,2,1,0:T(8,128)S(1)}, f32[8,16,32,128]{3,2,1,0:T(8,128)}, u32[]{:S(2)}) %copy-start.1) | copy-done | bytes 2097176
  84.4 0.0 copy-start.2
  84.4 1.6 %copy-done.2 = f32[8,16,32,128]{3,2,1,0:T(8,128)S(1)} copy-done((f32[8,16,32,128]{3,2,1,0:T(8,128)S(1)}, f32[8,16,32,128]{3,2,1,0:T(8,128)}, u32[]{:S(2)}) %copy-start.2) | copy-done | bytes 2097176
  86.0 0.0 copy-start.3
  86.0 0.7 copy-done.3
  86.7 7.2 %combine.1 = (f32[8,16,32,128]{3,2,1,0:T(8,128)}, f32[8,16,32,128]{3,2,1,0:T(8,128)}) custom-call(f32[2,8,128]{2,1,0:T(8,128)S(1)} %copy-done.3, f32[8,16,32,128]{3,2,1,0:T(8,128)S(1)} %copy-done, f32[8,16,32,128]{3,2,1,0:T(8,128)S(1)} %copy-done.1, f32[8,16,32,128]{3,2,1,0:T(8,128)S(1)} %copy-done.2), custom_call_target="tpu_custom_call" | custom-call | tf_op jit(solution)/shard_map/combine/pallas_call | solution.py:425
Async XLA Ops:
  0.6 82.2 %copy-start = (f32[8,16,32,128]{3,2,1,0:T(8,128)S(1)}, f32[8,16,32,128]{3,2,1,0:T(8,128)}, u32[]{:S(2)}) copy-start(f32[8,16,32,128]{3,2,1,0:T(8,128)} %refs_1_.3) | copy-start | bytes 6291460
  82.8 1.6 %copy-start.1 = (f32[8,16,32,128]{3,2,1,0:T(8,128)S(1)}, f32[8,16,32,128]{3,2,1,0:T(8,128)}, u32[]{:S(2)}) copy-start(f32[8,16,32,128]{3,2,1,0:T(8,128)} %get-tuple-element.6.refs_2_) | copy-start | bytes 6291460
  84.4 1.6 %copy-start.2 = (f32[8,16,32,128]{3,2,1,0:T(8,128)S(1)}, f32[8,16,32,128]{3,2,1,0:T(8,128)}, u32[]{:S(2)}) copy-start(f32[8,16,32,128]{3,2,1,0:T(8,128)} %get-tuple-element.7.refs_3_) | copy-start | bytes 6291460
  86.0 0.7 copy-start.3

commit v2 on v1

--- a/solution.py
+++ b/solution.py
@@ -124,30 +124,47 @@
         for f in items:
             f()
 
-    def y_faces(buf):
+    def y_faces(buf, start, length):
+        xs_ = pl.ds(start, length)
         return [
-            shift("gy", True, buf.at[:, :, pl.ds(ny, 8)], buf.at[:, :, pl.ds(0, 8)]),
-            shift("gy", False, buf.at[:, :, pl.ds(8, 8)], buf.at[:, :, pl.ds(ny + 8, 8)]),
+            shift("gy", True, buf.at[:, xs_, pl.ds(ny, 8)], buf.at[:, xs_, pl.ds(0, 8)]),
+            shift("gy", False, buf.at[:, xs_, pl.ds(8, 8)], buf.at[:, xs_, pl.ds(ny + 8, 8)]),
         ]
 
-    def pack(buf, depth, first, which):
-        n = len(which)
-
-        def take(k_x, yb):
-            if which is ALL:
-                return buf[:, k_x, yb * 8 : yb * 8 + 8]
-            return jnp.concatenate([buf[k : k + 1, k_x, yb * 8 : yb * 8 + 8] for k in which], axis=0)
-
-        def body(x, acc):
+    def w_faces(start, length, edge):
+        xs_ = pl.ds(start, length)
+        out = []
+        for b, up, src, dst in ((1, True, ny, 0), (-1, False, 8, ny + 8)):
+            for lo, hi in runs([k for k, o in enumerate(FORWARD) if o[1] == b and (o[0] or not edge)]):
+                ks = pl.ds(lo, hi - lo)
+                out.append(shift("gy", up, w.at[ks, xs_, pl.ds(src, 8)], w.at[ks, xs_, pl.ds(dst, 8)]))
+        return out
+
+    OWN = (1, nx, 1)
+    EDGE = (0, 2, nx + 1)
+    W_EDGE = (0, 1, 1)
+
+    def pack(part, take_low, take_high, n_low, n_high):
+        first, depth, stride = part
+
+        def body(t, accs):
+            low, high = accs
+            x = first + t * stride
             for yb in range(tiles):
-                j = x * tiles + yb
-                v = pltpu.roll(take(x, yb), lax.rem(j + 128 - first, 128), 2)
-                acc = jnp.where((lane == j)[None], v, acc)
-            return acc
-
-        return lax.fori_loop(0, depth, body, jnp.zeros((n, 8, 128), F32))
-
-    ALL = list(range(nf))
+                j = t * tiles + yb
+                here = (lane == j)[None]
+                low = jnp.where(here, pltpu.roll(take_low(x, yb), lax.rem(j + 1, 128), 2), low)
+                high = jnp.where(here, pltpu.roll(take_high(x, yb), j, 2), high)
+            return low, high
+
+        return lax.fori_loop(0, depth, body,
+                             (jnp.zeros((n_low, 8, 128), F32), jnp.zeros((n_high, 8, 128), F32)))
+
+    def of(ks):
+        def take(x, yb):
+            return jnp.concatenate([w[k : k + 1, x, yb * 8 : yb * 8 + 8] for k in ks], axis=0)
+
+        return take
 
     def gram(g, u, v):
         def body(x, accs):
@@ -177,26 +194,67 @@
     def own(buf):
         return lambda x, yb: buf[:, x + 1, 8 + yb * 8 : 16 + yb * 8]
 
-    def z_send(buf, e):
-        zsend[e, 0] = pack(buf, nx + 2, 127, ALL)
-        zsend[e, 1] = pack(buf, nx + 2, 0, ALL)
+    def z_send(buf, e, part):
+        p = 0 if part is OWN else 1
+
+        def take(x, yb):
+            return buf[:, x, yb * 8 : yb * 8 + 8]
+
+        low, high = pack(part, take, take, nf, nf)
+        zsend[e, p, 0] = low
+        zsend[e, p, 1] = high
         return [
-            shift("gz", True, zsend.at[e, 0], zrecv.at[e, 0]),
-            shift("gz", False, zsend.at[e, 1], zrecv.at[e, 1]),
+            shift("gz", True, zsend.at[e, p, 0], zrecv.at[e, p, 0]),
+            shift("gz", False, zsend.at[e, p, 1], zrecv.at[e, p, 1]),
         ]
 
-    def z_fill(buf, e):
-        def body(x, carry):
+    def w_send(part):
+        p = 0 if part is OWN else 1
+        low, high = pack(part, of(LO), of(HI), len(LO), len(HI))
+        wzsend[p, 0 : len(LO)] = low
+        wzsend[p, len(LO) : len(LO) + len(HI)] = high
+        lo_part, hi_part = pl.ds(0, len(LO)), pl.ds(len(LO), len(HI))
+        return [
+            shift("gz", True, wzsend.at[p, lo_part], wzrecv.at[p, lo_part]),
+            shift("gz", False, wzsend.at[p, hi_part], wzrecv.at[p, hi_part]),
+        ]
+
+    def z_fill(buf, e, part):
+        p = 0 if part is OWN else 1
+        first, depth, stride = part
+
+        def body(t, carry):
+            x = first + t * stride
             for yb in range(tiles):
-                j = x * tiles + yb
+                j = t * tiles + yb
                 v = buf[:, x, yb * 8 : yb * 8 + 8]
-                low = pltpu.roll(zrecv[e, 0], lax.rem(128 - j, 128), 2)
-                high = pltpu.roll(zrecv[e, 1], 127 - j, 2)
+                low = pltpu.roll(zrecv[e, p, 0], lax.rem(128 - j, 128), 2)
+                high = pltpu.roll(zrecv[e, p, 1], 127 - j, 2)
                 pm[:, x, yb * 8 : yb * 8 + 8] = jnp.where((lane == 0)[None], low, pltpu.roll(v, 1, 2))
                 pp[:, x, yb * 8 : yb * 8 + 8] = jnp.where((lane == 127)[None], high, pltpu.roll(v, 127, 2))
             return carry
 
-        lax.fori_loop(0, nx + 2, body, 0)
+        lax.fori_loop(0, depth, body, 0)
+
+    def w_fill(part):
+        p = 0 if part is OWN else 1
+        first, depth, stride = part
+
+        def body(t, carry):
+            x = first + t * stride
+            for yb in range(tiles):
+                j = t * tiles + yb
+                for n, k in enumerate(LO):
+                    v = pltpu.roll(w[k, x, yb * 8 : yb * 8 + 8], 1, 1)
+                    ws[k, x, yb * 8 : yb * 8 + 8] = jnp.where(
+                        lane == 0, pltpu.roll(wzrecv[p, n], lax.rem(128 - j, 128), 1), v)
+                for n, k in enumerate(HI):
+                    v = pltpu.roll(w[k, x, yb * 8 : yb * 8 + 8], 127, 1)
+                    ws[k, x, yb * 8 : yb * 8 + 8] = jnp.where(
+                        lane == 127, pltpu.roll(wzrecv[p, len(LO) + n], 127 - j, 1), v)
+            return carry
+
+        lax.fori_loop(0, depth, body, 0)
 
     def behind(k, x, yb):
         a, b, c = FORWARD[k]
@@ -206,10 +264,11 @@
     def ahead(k, x, yb):
         return w[k, x + 1, 8 + yb * 8 : 16 + yb * 8]
 
-    def stencil(buf, put):
+    def stencil(buf, put, first, depth, stride):
         views = {0: buf, -1: pm, 1: pp}
 
-        def body(x, carry):
+        def body(t, carry):
+            x = first + t * stride
             for yb in range(yb_n):
                 y = 8 + yb * 8
                 acc = diag[x, yb * 8 : yb * 8 + 8][None] * buf[:, x + 1, y : y + 8]
@@ -219,7 +278,7 @@
                 put(x, yb, acc)
             return carry
 
-        lax.fori_loop(0, nx, body, 0)
+        lax.fori_loop(0, depth, body, 0)
 
     k0, k1 = EX[0], EX[-1] + 1
     phase = [
@@ -227,43 +286,6 @@
         shift("gx", False, rhs.at[:, 0], p0.at[:, nx + 1, ys]),
         shift("gx", True, sten.at[pl.ds(k0 + 1, k1 - k0), nx - 1], w.at[pl.ds(k0, k1 - k0), 0, ys]),
     ]
-    loads[0].wait()
-    gram(0, own(p0), own(p0))
-    loads[1].wait()
-    loads[2].wait()
-    finish_all(phase)
-    phase = y_faces(p0)
-    for b, up, src, dst in ((1, True, ny, 0), (-1, False, 8, ny + 8)):
-        for lo, hi in runs([k for k, o in enumerate(FORWARD) if o[1] == b]):
-            ks = pl.ds(lo, hi - lo)
-            phase.append(shift("gy", up, w.at[ks, :, pl.ds(src, 8)], w.at[ks, :, pl.ds(dst, 8)]))
-    finish_all(phase)
-    phase = z_send(p0, 0)
-    wzsend[0 : len(LO)] = pack(w, nx + 1, 127, LO)
-    wzsend[len(LO) : len(LO) + len(HI)] = pack(w, nx + 1, 0, HI)
-    lo_part, hi_part = pl.ds(0, len(LO)), pl.ds(len(LO), len(HI))
-    phase += [
-        shift("gz", True, wzsend.at[lo_part], wzrecv.at[lo_part]),
-        shift("gz", False, wzsend.at[hi_part], wzrecv.at[hi_part]),
-    ]
-    finish_all(phase)
-    z_fill(p0, 0)
-
-    def w_fill(x, carry):
-        for yb in range(tiles):
-            j = x * tiles + yb
-            for n, k in enumerate(LO):
-                v = pltpu.roll(w[k, x, yb * 8 : yb * 8 + 8], 1, 1)
-                ws[k, x, yb * 8 : yb * 8 + 8] = jnp.where(
-                    lane == 0, pltpu.roll(wzrecv[n], lax.rem(128 - j, 128), 1), v)
-            for n, k in enumerate(HI):
-                v = pltpu.roll(w[k, x, yb * 8 : yb * 8 + 8], 127, 1)
-                ws[k, x, yb * 8 : yb * 8 + 8] = jnp.where(
-                    lane == 127, pltpu.roll(wzrecv[len(LO) + n], 127 - j, 1), v)
-        return carry
-
-    lax.fori_loop(0, nx + 1, w_fill, 0)
-
     def make_diag(x, carry):
         for yb in range(yb_n):
             total = s0[x, yb * 8 : yb * 8 + 8]
@@ -272,13 +294,48 @@
             diag[x, yb * 8 : yb * 8 + 8] = total
         return carry
 
-    lax.fori_loop(0, nx, make_diag, 0)
-
     def put_q1(x, yb, v):
         q0[:, x + 1, 8 + yb * 8 : 16 + yb * 8] = v
 
-    stencil(p0, put_q1)
-
+    def put_q2(x, yb, v):
+        q2[:, x, yb * 8 : yb * 8 + 8] = v
+
+    half = (nx - 2) // 2
+
+    def operate(buf, e, put, crossing):
+        finish_all(crossing)
+        ends = y_faces(buf, 0, 1) + y_faces(buf, nx + 1, 1)
+        if e == 0:
+            ends += w_faces(0, 1, True)
+        stencil(buf, put, 1, half, 1)
+        finish_all(ends)
+        ends = z_send(buf, e, EDGE)
+        if e == 0:
+            ends += w_send(W_EDGE)
+        stencil(buf, put, 1 + half, nx - 2 - half, 1)
+        finish_all(ends)
+        z_fill(buf, e, EDGE)
+        if e == 0:
+            w_fill(W_EDGE)
+            lax.fori_loop(0, 1, make_diag, 0)
+        stencil(buf, put, 0, 2, nx - 1)
+
+    loads[0].wait()
+    sides = y_faces(p0, 1, nx)
+    loads[1].wait()
+    sides += w_faces(1, nx, False)
+    gram(0, own(p0), own(p0))
+    loads[2].wait()
+    finish_all(sides)
+    sides = z_send(p0, 0, OWN)
+    sides += w_send(OWN)
+    finish_all(sides)
+    z_fill(p0, 0, OWN)
+    w_fill(OWN)
+    lax.fori_loop(1, nx, make_diag, 0)
+    operate(p0, 0, put_q1, phase)
+
+    sides = y_faces(q0, 1, nx)
     phase = [
         shift("gx", True, q0.at[:, nx, ys], q0.at[:, 0, ys]),
         shift("gx", False, q0.at[:, 1, ys], q0.at[:, nx + 1, ys]),
@@ -286,18 +343,12 @@
     save1 = pltpu.make_async_copy(q0.at[:, pl.ds(1, nx), ys], q1_out, lsem.at[3])
     save1.start()
     gram(1, own(p0), own(q0))
-    finish_all(phase)
-    phase = y_faces(q0)
-    finish_all(phase)
-    phase = z_send(q0, 1)
+    finish_all(sides)
+    sides = z_send(q0, 1, OWN)
     gram(2, own(q0), own(q0))
-    finish_all(phase)
-    z_fill(q0, 1)
-
-    def put_q2(x, yb, v):
-        q2[:, x, yb * 8 : yb * 8 + 8] = v
-
-    stencil(q0, put_q2)
+    finish_all(sides)
+    z_fill(q0, 1, OWN)
+    operate(q0, 1, put_q2, phase)
     save2 = pltpu.make_async_copy(q2, q2_out, lsem.at[4])
     save2.start()
     gram(3, own(q0), lambda x, yb: q2[:, x, yb * 8 : yb * 8 + 8])
@@ -395,10 +446,10 @@
             pltpu.VMEM((nx, ny, nz), F32),
             pltpu.VMEM((nx, ny, nz), F32),
             pltpu.VMEM((nf, nx, ny, nz), F32),
-            pltpu.VMEM((2, 2, nf, 8, nz), F32),
-            pltpu.VMEM((2, 2, nf, 8, nz), F32),
-            pltpu.VMEM((len(LO) + len(HI), 8, nz), F32),
-            pltpu.VMEM((len(LO) + len(HI), 8, nz), F32),
+            pltpu.VMEM((2, 2, 2, nf, 8, nz), F32),
+            pltpu.VMEM((2, 2, 2, nf, 8, nz), F32),
+            pltpu.VMEM((2, len(LO) + len(HI), 8, nz), F32),
+            pltpu.VMEM((2, len(LO) + len(HI), 8, nz), F32),
             pltpu.VMEM((8, 8, 128), F32),
             pltpu.VMEM((8, 128), F32),
             pltpu.VMEM((3, 8, 128), F32),
@@ -406,8 +457,8 @@
             pltpu.VMEM((sizes["gy"], 8, 128), F32),
             pltpu.VMEM((sizes["gz"], 8, 128), F32),
             pltpu.SemaphoreType.DMA((5,)),
-            pltpu.SemaphoreType.DMA((24,)),
-            pltpu.SemaphoreType.DMA((24,)),
+            pltpu.SemaphoreType.DMA((40,)),
+            pltpu.SemaphoreType.DMA((40,)),
             pltpu.SemaphoreType.DMA((peers,)),
             pltpu.SemaphoreType.DMA((peers,)),
         ],
@@ -429,7 +480,7 @@
         in_specs=[pl.BlockSpec(memory_space=pltpu.SMEM), block, block, block],
         out_specs=(block, block),
         scratch_shapes=[pltpu.VMEM((2, 8, 8, 8, 128), F32)],
-        compiler_params=pltpu.CompilerParams(dimension_semantics=("arbitrary",), vmem_limit_bytes=32 * 2**20),
+        compiler_params=pltpu.CompilerParams(dimension_semantics=("arbitrary",), vmem_limit_bytes=60 * 2**20),
         name="combine",
     )(c, rhs, q1, q2)
 

time: 94.1 us -> 72.3 us (0.77)
  Pallas kernels: 89.4 us -> 71.4 us
  local copies, waits for them, and re-layouts: 3.88 us -> 0 us
    pallas_call x1, Pallas kernels: 82.2 us -> 62.2 us  [shards(): pl.pallas_call(kernel, out_shape=(field, field, jax.ShapeDtypeStruct((2,...]
    unnamed x8 -> x0, local copies, waits for them, and re-layouts: 3.88 us -> none
    pallas_call x1, Pallas kernels: 7.21 us -> 9.23 us  [shards(): pl.pallas_call(last, grid=(nx // step,), out_shape=(field, field), in_spe...]
where the time goes in v2:
time: 72.3 us; the launch traced here: 72 us
  Pallas kernels  71.4 us (99%)
    pallas_call x1, Pallas kernels, shards(): pl.pallas_call(kernel, out_shape=(field, field, jax.ShapeDtypeStruct((2,...  62.2 us
    pallas_call x1, Pallas kernels, shards(): pl.pallas_call(last, grid=(nx // step,), out_shape=(field, field), in_spe...  9.23 us

profile of v2, /device:TPU:0, one launch (start us, length us, event | category | flops | bytes accessed | tf_op | source)
XLA Modules:
  0.0 72.0 jit_solution(5664067691000810710)
XLA Ops:
  0.6 62.2 %krylov.1 = (f32[8,16,32,128]{3,2,1,0:T(8,128)}, f32[8,16,32,128]{3,2,1,0:T(8,128)}, f32[2,8,128]{2,1,0:T(8,128)}) custom-call(f32[8,16,32,128]{3,2,1,0:T(8,128)} %refs_1_.3, f32[14,16,32,128]{3,2,1,0:T(8,128)} %refs_1_.2), custom_call_target="tpu_custom_call" | custom-call | tf_op jit(solution)/shard_map/krylov/pallas_call | solution.py:437
  62.8 9.2 %combine.1 = (f32[8,16,32,128]{3,2,1,0:T(8,128)}, f32[8,16,32,128]{3,2,1,0:T(8,128)}) custom-call(f32[2,8,128]{2,1,0:T(8,128)} %get-tuple-element.5.refs_0_, f32[8,16,32,128]{3,2,1,0:T(8,128)} %refs_1_.3, f32[8,16,32,128]{3,2,1,0:T(8,128)} %get-tuple-element.6.refs_2_, f32[8,16,32,128]{3,2,1,0:T(8,128)} %get-tuple-element.7.refs_3_), custom_call_target="tpu_custom_call" | custom-call | tf_op jit(solution)/shard_map/combine/pallas_call | solution.py:476

commit v3 on v2

--- a/solution.py
+++ b/solution.py
@@ -49,7 +49,7 @@
 
 
 def main_kernel(sizes, dims, rhs, sten, q1_out, q2_out, c_out, p0, q0, pm, pp, w, ws, s0, diag, q2,
-                zsend, zrecv, wzsend, wzrecv, red, gacc, cur, slot_x, slot_y, slot_z, lsem,
+                zsend, zrecv, wzsend, wzrecv, red, gacc, gsum, cur, slot_x, slot_y, slot_z, lsem,
                 xs, xr, ars, arr):
     nf, nx, ny = dims
     yb_n = ny // 8
@@ -186,7 +186,7 @@
             out = out + jnp.where(lane == 8 * g + i, t, 0.0)
             line = jnp.sum(jnp.where(lane == 8 * g + row, t, 0.0), axis=0, keepdims=True)
             out = out + jnp.where((row == i) & (lane > 8 * g + i), line, 0.0)
-        if g == 0:
+        if g in (0, 3):
             gacc[...] = out
         else:
             gacc[...] += out
@@ -280,6 +280,40 @@
 
         lax.fori_loop(0, depth, body, 0)
 
+    all_slots = (slot_y, slot_x, slot_z)
+    bases = [0]
+    for a in ("gy", "gx"):
+        bases.append(bases[-1] + sizes[a] - 1)
+
+    def sum_start(r, stage, value):
+        a = ("gy", "gx", "gz")[stage]
+        slots = all_slots[stage]
+        n = sizes[a]
+        i = pos[a]
+        cur[r, stage] = value
+        slots[r, i] = value
+
+        def copy(d, dst):
+            m = bases[stage] + d - 1
+            return pltpu.make_async_remote_copy(
+                src_ref=cur.at[r, stage], dst_ref=slots.at[r, dst],
+                send_sem=ars.at[r, m], recv_sem=arr.at[r, m],
+                device_id={a: lax.rem(i + d, n)}, device_id_type=pl.DeviceIdType.MESH)
+
+        for d in range(1, n):
+            copy(d, i).start()
+
+        def finish():
+            for d in range(1, n):
+                copy(d, i).wait_send()
+                copy(d, lax.rem(i + n - d, n)).wait_recv()
+            total = slots[r, 0]
+            for q in range(1, n):
+                total = total + slots[r, q]
+            return total
+
+        return finish
+
     k0, k1 = EX[0], EX[-1] + 1
     phase = [
         shift("gx", True, rhs.at[:, nx - 1], p0.at[:, 0, ys]),
@@ -300,19 +334,54 @@
     def put_q2(x, yb, v):
         q2[:, x, yb * 8 : yb * 8 + 8] = v
 
-    half = (nx - 2) // 2
-
-    def operate(buf, e, put, crossing):
+    def stencil_pairs(buf, put, first, pairs):
+        views = {0: buf, -1: pm, 1: pp}
+
+        def body(t, carry):
+            x = first + 2 * t
+            for yb in range(yb_n):
+                y = 8 + yb * 8
+                accs = [None, None]
+                for dx in (-1, 0, 1, 2):
+                    for dy in (-1, 0, 1):
+                        for dz in (-1, 0, 1):
+                            v = views[dz][:, x + 1 + dx, y + dy : y + dy + 8]
+                            for plane in (0, 1):
+                                o = (dx - plane, dy, dz)
+                                if abs(o[0]) > 1:
+                                    continue
+                                if o == (0, 0, 0):
+                                    coef = -diag[x + plane, yb * 8 : yb * 8 + 8]
+                                elif o > (0, 0, 0):
+                                    coef = ahead(FORWARD.index(o), x + plane, yb)
+                                else:
+                                    back = (-o[0], -o[1], -o[2])
+                                    coef = behind(FORWARD.index(back), x + plane, yb)
+                                term = coef[None] * v
+                                accs[plane] = -term if accs[plane] is None else accs[plane] - term
+                for plane in (0, 1):
+                    put(x + plane, yb, accs[plane])
+            return carry
+
+        lax.fori_loop(0, pairs, body, 0)
+
+    half = (nx - 2) // 4
+
+    def operate(buf, e, put, crossing, hooks=()):
         finish_all(crossing)
         ends = y_faces(buf, 0, 1) + y_faces(buf, nx + 1, 1)
         if e == 0:
             ends += w_faces(0, 1, True)
-        stencil(buf, put, 1, half, 1)
+        stencil_pairs(buf, put, 1, half)
+        if hooks:
+            hooks[0]()
         finish_all(ends)
         ends = z_send(buf, e, EDGE)
         if e == 0:
             ends += w_send(W_EDGE)
-        stencil(buf, put, 1 + half, nx - 2 - half, 1)
+        stencil_pairs(buf, put, 1 + 2 * half, (nx - 2) // 2 - half)
+        if hooks:
+            hooks[1]()
         finish_all(ends)
         z_fill(buf, e, EDGE)
         if e == 0:
@@ -346,51 +415,41 @@
     finish_all(sides)
     sides = z_send(q0, 1, OWN)
     gram(2, own(q0), own(q0))
+    pending = [sum_start(0, 0, gacc[...])]
     finish_all(sides)
     z_fill(q0, 1, OWN)
-    operate(q0, 1, put_q2, phase)
+    pending.append(sum_start(0, 1, pending[0]()))
+
+    def hook_a():
+        pending.append(sum_start(0, 2, pending[1]()))
+
+    def hook_b():
+        gsum[...] = pending[2]()
+
+    operate(q0, 1, put_q2, phase, (hook_a, hook_b))
     save2 = pltpu.make_async_copy(q2, q2_out, lsem.at[4])
     save2.start()
     gram(3, own(q0), lambda x, yb: q2[:, x, yb * 8 : yb * 8 + 8])
 
-    total = gacc[...]
-    base = 0
-    for stage, (a, slots) in enumerate(zip(("gy", "gx", "gz"), (slot_y, slot_x, slot_z))):
-        n = sizes[a]
-        i = pos[a]
-        cur[stage] = total
-        slots[i] = total
-        copies = []
-        for d in range(1, n):
-            copies.append(pltpu.make_async_remote_copy(
-                src_ref=cur.at[stage], dst_ref=slots.at[i],
-                send_sem=ars.at[base + d - 1], recv_sem=arr.at[base + d - 1],
-                device_id={a: lax.rem(i + d, n)}, device_id_type=pl.DeviceIdType.MESH))
-        for copy in copies:
-            copy.start()
-        for d, copy in zip(range(1, n), copies):
-            copy.wait_send()
-            pltpu.make_async_remote_copy(
-                src_ref=cur.at[stage], dst_ref=slots.at[lax.rem(i + n - d, n)],
-                send_sem=ars.at[base + d - 1], recv_sem=arr.at[base + d - 1],
-                device_id={a: lax.rem(i + d, n)}, device_id_type=pl.DeviceIdType.MESH).wait_recv()
-        total = slots[0]
-        for s in range(1, n):
-            total = total + slots[s]
-        base += n - 1
-
+    done = sum_start(1, 0, gacc[...])
+    total = gsum[...]
     small = lane < 8
-    parts = [jnp.where(small, pltpu.roll(total, (128 - 8 * g) % 128, 1), 0.0) for g in range(4)]
-    rr, pq, ss, tt = parts
+    parts = [jnp.where(small, pltpu.roll(total, (128 - 8 * g) % 128, 1), 0.0) for g in range(3)]
+    rr, pq, ss = parts
     alpha = jnp.where(small, solve(pq, rr, row), 0.0)
+    done = sum_start(1, 1, done())
     alpha_t = transposed(alpha, row, lane)
     alpha_t = jnp.where(small, alpha_t, 0.0)
     ssa = mm(ss, alpha)
     new = rr - mm(alpha_t, pq) - mm(pq, alpha) + mm(alpha_t, ssa)
     beta = jnp.where(small, solve(rr, new, row), 0.0)
+    done = sum_start(1, 2, done())
     ib = beta + jnp.where(lane == row, 1.0, 0.0)
     ib_t = jnp.where(small, transposed(ib, row, lane), 0.0)
-    curve = mm(ib_t, mm(pq, ib) - ssa) - mm(alpha_t, mm(ss, ib) - mm(tt, alpha))
+    left = mm(ib_t, mm(pq, ib) - ssa)
+    mid = mm(ss, ib)
+    tt = jnp.where(small, pltpu.roll(done(), 128 - 24, 1), 0.0)
+    curve = left - mm(alpha_t, mid - mm(tt, alpha))
     alpha1 = jnp.where(small, solve(curve, new, row), 0.0)
     c_out[0] = alpha + mm(ib, alpha1)
     c_out[1] = mm(alpha, alpha1)
@@ -452,15 +511,16 @@
             pltpu.VMEM((2, len(LO) + len(HI), 8, nz), F32),
             pltpu.VMEM((8, 8, 128), F32),
             pltpu.VMEM((8, 128), F32),
-            pltpu.VMEM((3, 8, 128), F32),
-            pltpu.VMEM((sizes["gx"], 8, 128), F32),
-            pltpu.VMEM((sizes["gy"], 8, 128), F32),
-            pltpu.VMEM((sizes["gz"], 8, 128), F32),
+            pltpu.VMEM((8, 128), F32),
+            pltpu.VMEM((2, 3, 8, 128), F32),
+            pltpu.VMEM((2, sizes["gx"], 8, 128), F32),
+            pltpu.VMEM((2, sizes["gy"], 8, 128), F32),
+            pltpu.VMEM((2, sizes["gz"], 8, 128), F32),
             pltpu.SemaphoreType.DMA((5,)),
             pltpu.SemaphoreType.DMA((40,)),
             pltpu.SemaphoreType.DMA((40,)),
-            pltpu.SemaphoreType.DMA((peers,)),
-            pltpu.SemaphoreType.DMA((peers,)),
+            pltpu.SemaphoreType.DMA((2, peers)),
+            pltpu.SemaphoreType.DMA((2, peers)),
         ],
         compiler_params=pltpu.CompilerParams(
             collective_id=0, has_side_effects=True, vmem_limit_bytes=60 * 2**20),

time: 72.3 us -> 71.7 us (level)
  no operation moved by 1% of the time
where the time goes in v3:
time: 71.7 us; the launch traced here: 71.4 us
  Pallas kernels  70.7 us (99%)
    pallas_call x1, Pallas kernels, shards(): pl.pallas_call(kernel, out_shape=(field, field, jax.ShapeDtypeStruct((2,...  61.5 us
    pallas_call x1, Pallas kernels, shards(): pl.pallas_call(last, grid=(nx // step,), out_shape=(field, field), in_spe...  9.23 us

profile of v3, /device:TPU:0, one launch (start us, length us, event | category | flops | bytes accessed | tf_op | source)
XLA Modules:
  0.0 71.4 jit_solution(12013788215581858945)
XLA Ops:
  0.6 61.5 %krylov.1 = (f32[8,16,32,128]{3,2,1,0:T(8,128)}, f32[8,16,32,128]{3,2,1,0:T(8,128)}, f32[2,8,128]{2,1,0:T(8,128)}) custom-call(f32[8,16,32,128]{3,2,1,0:T(8,128)} %refs_1_.3, f32[14,16,32,128]{3,2,1,0:T(8,128)} %refs_1_.2), custom_call_target="tpu_custom_call" | custom-call | tf_op jit(solution)/shard_map/krylov/pallas_call | solution.py:496
  62.1 9.2 %combine.1 = (f32[8,16,32,128]{3,2,1,0:T(8,128)}, f32[8,16,32,128]{3,2,1,0:T(8,128)}) custom-call(f32[2,8,128]{2,1,0:T(8,128)} %get-tuple-element.5.refs_0_, f32[8,16,32,128]{3,2,1,0:T(8,128)} %refs_1_.3, f32[8,16,32,128]{3,2,1,0:T(8,128)} %get-tuple-element.6.refs_2_, f32[8,16,32,128]{3,2,1,0:T(8,128)} %get-tuple-element.7.refs_3_), custom_call_target="tpu_custom_call" | custom-call | tf_op jit(solution)/shard_map/combine/pallas_call | solution.py:536
